TPU v7x, 32 devices: a whole 2x2x4 slice. The times are simulated.
32 devices in a mesh: seq: 8 (over z, y), grp: 4 (over x, core).
Axes of the slice: x: 2, y: 2, z: 4, core: 2. Of those that a mesh axis runs over, the one named last changes fastest.
Arguments:
- frames: bfloat16 [16384, 1024], P(('seq', 'grp')), may hold values from -6 to 6
- ln1_gain: float32 [1024], replicated, may hold values from 0.1 to 1.9
- w_in: bfloat16 [1024, 2, 1024], P('seq', None, 'grp'), may hold values from -0.1875 to 0.1875
- w_dw: bfloat16 [31, 1024], replicated, may hold values from -1 to 1
- ln2_gain: float32 [1024], replicated, may hold values from 0.1 to 1.9
- ln2_bias: float32 [1024], replicated, may hold values from -3 to 3
- w_out: bfloat16 [1024, 1024], P('grp', 'seq'), may hold values from -0.1875 to 0.1875
- block_utt: int32 [128], replicated, may hold values from 0 to 31, as said below
- block_off: int32 [128], replicated, may hold values from 0 to 6, as said below
- lengths: int32 [32], replicated, may hold values from 1 to 896, as said below
Outputs:
- result: bfloat16 [16384, 1024], P(('seq', 'grp'))
Inputs may be any that keep to these rules, and one draw needn't show every extreme that they name: block_utt never falls along the blocks and names every utterance; each utterance is one run of 1 to 7 whole blocks, and some utterance has exactly 7. block_off counts the blocks of the run before a block, starting at 0. `lengths`: an utterance of n blocks has more than (n - 1) * 128 and at most n * 128 live frames.
All inputs are finite; a program needn't handle non-finite values.
Results may differ from a plain program's by a relative error of at most 0.0046.
Values may be sent and summed in bfloat16 or wider, within the bound.
A program may use at most 64 MiB of HBM per device.

v0:
```python
import functools

import jax
import jax.numpy as jnp
from jax import lax
from jax.experimental import pallas as pl
from jax.experimental.pallas import tpu as pltpu
from jax.sharding import PartitionSpec as P

D = 1024
KER = 31
BLK = 128


epsilon = 1e-05


def extended(block, sides, width):
    for axis, dim in sides:
        count = lax.axis_size(axis)
        forward = [(i, i + 1) for i in range(count - 1)]
        backward = [(target, source) for source, target in forward]
        low = lax.ppermute(
            lax.slice_in_dim(block, block.shape[dim] - width, None, axis=dim), axis, forward
        )
        high = lax.ppermute(lax.slice_in_dim(block, 0, width, axis=dim), axis, backward)
        block = jnp.concatenate([low, block, high], axis=dim)
    return block


def frame_keys(block_utt, block_off, lengths, first_row, row_count, margin):
    places = first_row - margin + jnp.arange(row_count + 2 * margin, dtype=jnp.int32)
    total_rows = block_utt.shape[0] * BLK
    inside = (places >= 0) & (places < total_rows)
    blocks = jnp.clip(places // BLK, 0, block_utt.shape[0] - 1)
    utterance = jnp.take(block_utt, blocks)
    position = jnp.take(block_off, blocks) * BLK + places % BLK
    living = inside & (position < jnp.take(lengths, utterance))
    return (jnp.where(living, utterance, -1), living[margin : margin + row_count])


def layer_norm(rows, gain):
    values = rows.astype(jnp.float32)
    average = jnp.mean(values, axis=1, keepdims=True)
    centered = values - average
    spread = jnp.mean(centered * centered, axis=1, keepdims=True)
    return (centered * lax.rsqrt(spread + epsilon) * gain).astype(jnp.bfloat16)


def gate_units(projected, living):
    half = projected.shape[1] // 2
    values = projected[:, :half] * jax.nn.sigmoid(projected[:, half:])
    return (values * living.astype(jnp.float32)[:, None]).astype(jnp.bfloat16)


def depthwise(widened, keys_wide, taps, row_count):
    margin = (taps.shape[0] - 1) // 2
    center = keys_wide[margin : margin + row_count]
    summed = jnp.zeros((row_count, widened.shape[1]), jnp.float32)
    for tap_index in range(taps.shape[0]):
        shifted = widened[tap_index : tap_index + row_count].astype(jnp.float32)
        same = (keys_wide[tap_index : tap_index + row_count] == center)[:, None]
        summed = summed + jnp.where(same, shifted, 0.0) * taps[tap_index].astype(jnp.float32)
    return summed


def finish(mixed, stat_sum, square_sum, width_total, gain, bias):
    average = stat_sum / width_total
    spread = square_sum / width_total - average * average
    normed = (mixed - average[:, None]) * lax.rsqrt(spread + epsilon)[:, None] * gain + bias
    return (normed * jax.nn.sigmoid(normed)).astype(jnp.bfloat16)


def project_rows(normed, row_count, column_count):

    def add_rows(total, weight_piece, start_row):
        piece_rows = weight_piece.shape[0]
        return jnp.dot(
            normed, weight_piece.reshape(piece_rows, -1), preferred_element_type=jnp.float32
        )

    return (add_rows, jnp.zeros((row_count, column_count), jnp.float32))


def per_device(
    frames, ln1_gain, w_in, w_dw, ln2_gain, ln2_bias, w_out, block_utt, block_off, lengths
):
    row_count = frames.shape[0]
    margin = (KER - 1) // 2
    own_first = lax.axis_index(("seq", "grp")) * row_count
    keys_wide, living = frame_keys(block_utt, block_off, lengths, own_first, row_count, margin)
    normed = layer_norm(frames, ln1_gain)
    w_in_rows, w_out_rows = (
        lax.all_gather(w_in, "grp", axis=2, tiled=True),
        lax.all_gather(w_out, "grp", axis=0, tiled=True),
    )
    add_rows, empty = project_rows(normed, row_count, 2 * D)
    projected = add_rows(empty, lax.all_gather(w_in_rows, "seq", axis=0, tiled=True), jnp.int32(0))
    gated = gate_units(projected, living)
    widened = extended(gated, ((("seq", "grp"), 0),), margin)
    mixed = depthwise(widened, keys_wide, w_dw, row_count)
    act = finish(
        mixed, jnp.sum(mixed, axis=1), jnp.sum(mixed * mixed, axis=1), float(D), ln2_gain, ln2_bias
    )
    output = jnp.dot(
        act,
        lax.all_gather(w_out_rows, "seq", axis=1, tiled=True),
        preferred_element_type=jnp.float32,
    )
    alive = living.astype(jnp.float32)[:, None]
    return (frames.astype(jnp.float32) + output * alive).astype(jnp.bfloat16)


MESH = pl.DeviceIdType.MESH
HALO = 16
LANES = 128


def fused_kernel(
    nz,
    frames_hbm,
    wi_hbm,
    wo_hbm,
    gain1,
    taps,
    gain2,
    bias2,
    utts,
    offs,
    lens,
    out_hbm,
    WI,
    WO,
    FR,
    HB,
    NM,
    GB,
    MX,
    TP,
    ACT,
    OUT,
    ssem,
    rsem,
    hs,
    hr,
    lsem,
    osem,
):
    rows, width = FR.shape
    krows = wi_hbm.shape[0]
    orows, ocols = wo_hbm.shape
    nblk = rows // BLK
    chunks = width // LANES
    per_group = wi_hbm.shape[1] // (2 * LANES)
    seq = lax.axis_index("seq")
    grp = lax.axis_index("grp")
    nseq = lax.axis_size("seq")
    ngrp = lax.axis_size("grp")
    z, y = seq // 2, seq % 2
    x, c = grp // 2, grp % 2
    index = seq * ngrp + grp
    total = nseq * ngrp
    after = (index + 1) % total
    before = (index + total - 1) % total
    px = (seq, (1 - x) * 2 + c)
    py = (z * 2 + 1 - y, grp)
    pp = (seq, x * 2 + 1 - c)
    pn = (after // ngrp, after % ngrp)
    pb = (before // ngrp, before % ngrp)
    up = (jnp.minimum(z + 1, nz - 1) * 2 + y, grp)
    down = (jnp.maximum(z - 1, 0) * 2 + y, grp)
    has_up = z < nz - 1
    has_down = z > 0

    own_in = WI.at[grp, pl.ds(pl.multiple_of(seq * krows, krows), krows), :]
    own_out = WO.at[
        pl.ds(pl.multiple_of(grp * orows, orows), orows),
        pl.ds(pl.multiple_of(seq * ocols, ocols), ocols),
    ]
    load_in = pltpu.make_async_copy(wi_hbm, own_in, lsem.at[0])
    load_out = pltpu.make_async_copy(wo_hbm, own_out, lsem.at[1])
    load_fr = pltpu.make_async_copy(frames_hbm, FR, lsem.at[2])
    load_in.start()
    load_fr.start()
    load_out.start()

    barrier = pltpu.get_barrier_semaphore()
    for peer in (px, py, pp, pn, pb):
        pl.semaphore_signal(barrier, inc=1, device_id=peer, device_id_type=MESH)

    @pl.when(has_up)
    def _():
        pl.semaphore_signal(barrier, inc=1, device_id=up, device_id_type=MESH)

    @pl.when(has_down)
    def _():
        pl.semaphore_signal(barrier, inc=1, device_id=down, device_id_type=MESH)

    load_in.wait()
    pl.semaphore_wait(barrier, 5 + has_up.astype(jnp.int32) + has_down.astype(jnp.int32))

    def slot(w, sx, sy, sz, sc, half=None):
        g = sx * 2 + sc
        s = sz * 2 + sy
        if w == 0:
            count = krows if half is None else krows // 2
            first = s * krows + (0 if half is None else half * count)
            return WI.at[g, pl.ds(pl.multiple_of(first, count), count), :]
        count = orows if half is None else orows // 2
        first = g * orows + (0 if half is None else half * count)
        return WO.at[
            pl.ds(pl.multiple_of(first, count), count),
            pl.ds(pl.multiple_of(s * ocols, ocols), ocols),
        ]

    ZU, ZD = 0, nz - 1
    XD, YD = 2 * nz - 2, 3 * nz - 2
    XH, YH = 4 * nz - 2, 5 * nz - 2
    PO, PY, PX, PXH, PYH = (6 * nz - 2 + i * nz for i in range(5))

    def copy(w, ref, sem, dev):
        return pltpu.make_async_remote_copy(
            src_ref=ref,
            dst_ref=ref,
            send_sem=ssem.at[w, sem],
            recv_sem=rsem.at[w, sem],
            device_id=dev,
            device_id_type=MESH,
        )

    def spread(w, sz):
        ref = slot(w, x, y, sz, c)
        copy(w, ref, XD + sz, px).start()
        copy(w, ref, YD + sz, py).start()
        copy(w, ref, PO + sz, pp).start()

    def first_sends(w):
        ref = slot(w, x, y, z, c)

        @pl.when(has_up)
        def _():
            copy(w, ref, ZU, up).start()

        @pl.when(has_down)
        def _():
            copy(w, ref, ZD, down).start()

        spread(w, z)

    def line(w, d):
        @pl.when(z >= d)
        def _():
            ref = slot(w, x, y, z - d, c)
            copy(w, ref, ZU + d - 1, down).wait_recv()
            if d < nz - 1:

                @pl.when(has_up)
                def _():
                    copy(w, ref, ZU + d, up).start()

            spread(w, z - d)

        @pl.when(z + d < nz)
        def _():
            ref = slot(w, x, y, z + d, c)
            copy(w, ref, ZD + d - 1, up).wait_recv()
            if d < nz - 1:

                @pl.when(has_down)
                def _():
                    copy(w, ref, ZD + d, down).start()

            spread(w, z + d)

    def square_at(w, sz):
        ref = slot(w, x, 1 - y, sz, c)
        copy(w, ref, YD + sz, py).wait_recv()
        copy(w, slot(w, x, 1 - y, sz, c, 0), XH + sz, px).start()
        copy(w, ref, PY + sz, pp).start()
        ref = slot(w, 1 - x, y, sz, c)
        copy(w, ref, XD + sz, px).wait_recv()
        copy(w, slot(w, 1 - x, y, sz, c, 1), YH + sz, py).start()
        copy(w, ref, PX + sz, pp).start()

    def corner_at(w, sz):
        ref = slot(w, 1 - x, 1 - y, sz, c, 0)
        copy(w, ref, XH + sz, px).wait_recv()
        copy(w, ref, PXH + sz, pp).start()
        ref = slot(w, 1 - x, 1 - y, sz, c, 1)
        copy(w, ref, YH + sz, py).wait_recv()
        copy(w, ref, PYH + sz, pp).start()

    def at_distance(step, w, d):
        if d == 0:
            step(w, z)
            return

        @pl.when(z >= d)
        def _():
            step(w, z - d)

        @pl.when(z + d < nz)
        def _():
            step(w, z + d)

    def partner_near(w):
        for sz in range(nz):
            copy(w, slot(w, x, y, sz, 1 - c), PO + sz, pp).wait_recv()
            copy(w, slot(w, x, 1 - y, sz, 1 - c), PY + sz, pp).wait_recv()

    def partner_far(w):
        for sz in range(nz):
            copy(w, slot(w, 1 - x, y, sz, 1 - c), PX + sz, pp).wait_recv()
            copy(w, slot(w, 1 - x, 1 - y, sz, 1 - c, 0), PXH + sz, pp).wait_recv()
            copy(w, slot(w, 1 - x, 1 - y, sz, 1 - c, 1), PYH + sz, pp).wait_recv()

    def halo_copy(src, dst, sem, dev):
        return pltpu.make_async_remote_copy(
            src_ref=src,
            dst_ref=dst,
            send_sem=hs.at[sem],
            recv_sem=hr.at[sem],
            device_id=dev,
            device_id_type=MESH,
        )

    to_next = halo_copy(FR.at[pl.ds(rows - HALO, HALO), :], HB.at[0], 0, pn)
    to_before = halo_copy(FR.at[pl.ds(0, HALO), :], HB.at[1], 1, pb)

    first_sends(0)
    load_fr.wait()
    to_next.start()
    to_before.start()
    load_out.wait()
    first_sends(1)

    for ch in range(chunks):
        TP[ch, 0:KER, :] = taps[:, ch * LANES : (ch + 1) * LANES].astype(jnp.float32)

    def norm_rows(block):
        values = block.astype(jnp.float32)
        average = jnp.mean(values, axis=1, keepdims=True)
        centered = values - average
        spread_ = jnp.mean(centered * centered, axis=1, keepdims=True)
        return (centered * lax.rsqrt(spread_ + epsilon) * gain1[...]).astype(jnp.bfloat16)

    step_rows = 32

    def norm_step(i, carry):
        first = pl.multiple_of(i * step_rows, step_rows)
        NM[pl.ds(pl.multiple_of(first + HALO, HALO), step_rows), :] = norm_rows(
            FR[pl.ds(first, step_rows), :]
        )
        return carry

    lax.fori_loop(0, rows // step_rows, norm_step, 0)

    first_block = index * nblk
    last_block = total * nblk - 1

    def block_info(b):
        u = utts[b]
        return u, lens[u] - offs[b] * BLK

    info = [
        block_info(jnp.clip(first_block + i, 0, last_block)) for i in range(-1, nblk + 1)
    ]
    joined = []
    for i in range(nblk + 1):
        same = info[i][0] == info[i + 1][0]
        if i == 0:
            same = same & (first_block > 0)
        if i == nblk:
            same = same & (first_block + nblk <= last_block)
        joined.append(same.astype(jnp.float32))
    alive_rows = [info[i + 1][1] for i in range(nblk)]

    def tall(count, start):
        return start + lax.broadcasted_iota(jnp.int32, (count, LANES), 0)

    def project(g):
        def chunk_step(h, carry):
            weights = WI[g, :, pl.ds(pl.multiple_of(h * 2 * LANES, 2 * LANES), 2 * LANES)]
            p = jnp.dot(NM[...], weights, preferred_element_type=jnp.float32)
            half = 0.5 * p[:, :LANES]
            units = half + half * jnp.tanh(0.5 * p[:, LANES:])
            pieces = [
                jnp.where(tall(HALO, BLK - HALO) < info[0][1], units[:HALO], 0.0)
            ]
            for i in range(nblk):
                part = units[HALO + i * BLK : HALO + (i + 1) * BLK]
                pieces.append(jnp.where(tall(BLK, 0) < alive_rows[i], part, 0.0))
            pieces.append(
                jnp.where(tall(HALO, 0) < info[nblk + 1][1], units[HALO + rows :], 0.0)
            )
            pieces = [q.astype(jnp.bfloat16).astype(jnp.float32) for q in pieces]
            stride = BLK + 2 * HALO
            for i in range(nblk):
                base = i * stride
                GB[base : base + HALO, :] = pieces[i][-HALO:] * joined[i]
                GB[base + HALO : base + HALO + BLK, :] = pieces[i + 1]
                GB[base + HALO + BLK : base + stride, :] = pieces[i + 2][:HALO] * joined[i + 1]
            ch = g * per_group + h
            tap = [jnp.broadcast_to(TP[ch, k : k + 1, :], (8, LANES)) for k in range(KER)]
            deep = 4
            per_block = BLK // (8 * deep)

            def conv_step(j, inner):
                i, q = j // per_block, j % per_block
                base = pl.multiple_of(i * stride + q * (8 * deep), 8)
                sums = [None] * deep
                for o in range(8 * (deep - 1) + KER):
                    value = GB[pl.ds(base + (1 + o), 8), :]
                    for t in range(deep):
                        k = o - 8 * t
                        if 0 <= k < KER:
                            term = value * tap[k]
                            sums[t] = term if sums[t] is None else sums[t] + term
                first = pl.multiple_of(j * (8 * deep), 8 * deep)
                for t in range(deep):
                    MX[ch, pl.ds(pl.multiple_of(first + 8 * t, 8), 8), :] = sums[t]
                return inner

            lax.fori_loop(0, nblk * per_block, conv_step, 0, unroll=2)
            return carry

        lax.fori_loop(0, per_group, chunk_step, 0)

    line(0, 1)
    at_distance(square_at, 0, 0)
    line(1, 1)
    for d in range(2, nz):
        line(0, d)
        at_distance(square_at, 0, d - 1)
        line(1, d)
        at_distance(square_at, 1, d - 2)
    to_before.wait_recv()
    to_next.wait_recv()
    NM[0:HALO, :] = norm_rows(HB[0])
    NM[HALO + rows :, :] = norm_rows(HB[1])
    at_distance(square_at, 0, nz - 1)
    at_distance(square_at, 1, nz - 2)
    project(grp)
    at_distance(corner_at, 0, 0)
    at_distance(square_at, 1, nz - 1)
    partner_near(0)
    project(x * 2 + 1 - c)
    for d in range(1, nz):
        at_distance(corner_at, 0, d)
    at_distance(corner_at, 1, 0)
    project((1 - x) * 2 + c)
    partner_far(0)
    for d in range(1, nz - 1):
        at_distance(corner_at, 1, d)
    project((1 - x) * 2 + 1 - c)

    at_distance(corner_at, 1, nz - 1)

    def finish_step(j, carry):
        first = pl.multiple_of(j * step_rows, step_rows)
        parts = [MX[ch, pl.ds(first, step_rows), :] for ch in range(chunks)]
        s1 = parts[0]
        s2 = parts[0] * parts[0]
        for part in parts[1:]:
            s1 = s1 + part
            s2 = s2 + part * part
        average = jnp.sum(s1, axis=1, keepdims=True) / float(width)
        spread_ = jnp.sum(s2, axis=1, keepdims=True) / float(width) - average * average
        scale = lax.rsqrt(spread_ + epsilon)
        for ch in range(chunks):
            cols = slice(ch * LANES, (ch + 1) * LANES)
            v = (parts[ch] - average) * scale * gain2[:, cols] + bias2[:, cols]
            v = 0.5 * v
            ACT[pl.ds(first, step_rows), cols] = (v + v * jnp.tanh(v)).astype(jnp.bfloat16)
        return carry

    lax.fori_loop(0, rows // step_rows, finish_step, 0)

    partner_near(1)
    partner_far(1)

    wide = 2 * LANES

    def out_copy(n):
        cols = pl.ds(pl.multiple_of(n * wide, wide), wide)
        return pltpu.make_async_copy(OUT.at[:, cols], out_hbm.at[:, cols], osem.at[n])

    def out_step(n, carry):
        cols = pl.ds(pl.multiple_of(n * wide, wide), wide)
        o = jnp.dot(ACT[...], WO[:, cols], preferred_element_type=jnp.float32)
        for i in range(nblk):
            band = slice(i * BLK, (i + 1) * BLK)
            lived = (
                lax.broadcasted_iota(jnp.int32, (BLK, wide), 0) < alive_rows[i]
            ).astype(jnp.float32)
            out_hbm[band, cols] = (
                FR[band, cols].astype(jnp.float32) + o[band] * lived
            ).astype(jnp.bfloat16)
        return carry

    lax.fori_loop(0, width // wide, out_step, 0)

    to_next.wait_send()
    to_before.wait_send()
    for w in range(2):
        full = slot(w, x, y, z, c)
        part = slot(w, x, y, z, c, 0)
        for d in range(1, nz):

            @pl.when((z >= d - 1) & has_up)
            def _():
                copy(w, full, ZU + d - 1, up).wait_send()

            @pl.when((z + d - 1 < nz) & has_down)
            def _():
                copy(w, full, ZD + d - 1, down).wait_send()

        for sz in range(nz):
            copy(w, full, XD + sz, px).wait_send()
            copy(w, full, YD + sz, py).wait_send()
            copy(w, part, XH + sz, px).wait_send()
            copy(w, part, YH + sz, py).wait_send()
            copy(w, full, PO + sz, pp).wait_send()
            copy(w, full, PY + sz, pp).wait_send()
            copy(w, full, PX + sz, pp).wait_send()
            copy(w, part, PXH + sz, pp).wait_send()
            copy(w, part, PYH + sz, pp).wait_send()


def fused_device(
    frames, ln1_gain, w_in, w_dw, ln2_gain, ln2_bias, w_out, block_utt, block_off, lengths
):
    rows, width = frames.shape
    nz = lax.axis_size("seq") // 2
    krows, _, cols = w_in.shape
    groups = cols // LANES
    wi = w_in.reshape(krows, 2, groups, LANES).transpose(0, 2, 1, 3).reshape(krows, 2 * cols)
    vmem = pl.BlockSpec(memory_space=pltpu.VMEM)
    smem = pl.BlockSpec(memory_space=pltpu.SMEM)
    anywhere = pl.BlockSpec(memory_space=pl.ANY)
    nsem = 11 * nz - 2
    nblk = rows // BLK
    return pl.pallas_call(
        functools.partial(fused_kernel, nz),
        out_shape=jax.ShapeDtypeStruct((rows, width), jnp.bfloat16),
        in_specs=[anywhere] * 3 + [vmem] * 4 + [smem] * 3,
        out_specs=vmem,
        scratch_shapes=[
            pltpu.VMEM((width // cols, width, 2 * cols), jnp.bfloat16),
            pltpu.VMEM((width, width), jnp.bfloat16),
            pltpu.VMEM((rows, width), jnp.bfloat16),
            pltpu.VMEM((2, HALO, width), jnp.bfloat16),
            pltpu.VMEM((rows + 2 * HALO, width), jnp.bfloat16),
            pltpu.VMEM((nblk * (BLK + 2 * HALO), LANES), jnp.float32),
            pltpu.VMEM((width // LANES, rows, LANES), jnp.float32),
            pltpu.VMEM((width // LANES, 32, LANES), jnp.float32),
            pltpu.VMEM((rows, width), jnp.bfloat16),
            pltpu.VMEM((rows, width), jnp.bfloat16),
            pltpu.SemaphoreType.DMA((2, nsem)),
            pltpu.SemaphoreType.DMA((2, nsem)),
            pltpu.SemaphoreType.DMA((2,)),
            pltpu.SemaphoreType.DMA((2,)),
            pltpu.SemaphoreType.DMA((3,)),
            pltpu.SemaphoreType.DMA((width // (2 * LANES),)),
        ],
        compiler_params=pltpu.CompilerParams(
            collective_id=0, has_side_effects=True, vmem_limit_bytes=40 << 20
        ),
    )(
        frames,
        wi,
        w_out,
        ln1_gain[None],
        w_dw,
        ln2_gain[None],
        ln2_bias[None],
        block_utt,
        block_off,
        lengths,
    )


def solution(mesh):
    seq, grp = mesh.shape["seq"], mesh.shape["grp"]
    fits = grp == 4 and seq % 2 == 0 and 4 <= seq <= 8 and D % (seq * LANES) == 0

    return jax.shard_map(
        fused_device if fits else per_device,
        mesh=mesh,
        in_specs=(
            P(("seq", "grp"), None),
            P(),
            P("seq", None, "grp"),
            P(),
            P(),
            P(),
            P("grp", "seq"),
            P(),
            P(),
            P(),
        ),
        out_specs=P(("seq", "grp"), None),
        check_vma=False,
    )
```

profile of v0, /device:TPU:0, one launch (start us, length us, event | category | flops | bytes accessed | tf_op | source)
XLA Modules:
  0.0 46.8 jit_solution(160468280698549806)
XLA Ops:
  0.0 0.0 copy-start.1
  0.0 0.0 copy-start.2
  0.0 0.0 copy-start.3
  0.0 0.0 copy-start.4
  0.0 0.0 copy-start.5
  0.0 0.0 copy-start.6
  0.0 0.0 copy-start.7
  0.0 0.0 copy-start.8
  0.0 1.1 %reshape.7.wi_hbm = bf16[128,512]{1,0:T(8,128)(2,1)S(1)} reshape(bf16[128,2,2,128]{3,2,1,0:T(2,128)(2,1)} %bitcast.9) | data formatting | bytes 262144 | tf_op jit(solution)/shard_map/reshape | solution.py:537
  1.1 0.0 copy-done.1
  1.1 0.0 copy-done.2
  1.1 0.0 copy-done.3
  1.2 0.0 copy-done.4
  1.2 0.0 copy-done.5
  1.2 0.0 copy-done.6
  1.2 0.0 copy-done.7
  1.2 0.0 copy-done.8
  1.2 0.0 copy-start
  1.2 1.2 %copy-done = bf16[512,1024]{1,0:T(8,128)(2,1)S(1)} copy-done((bf16[512,1024]{1,0:T(8,128)(2,1)S(1)}, bf16[512,1024]{1,0:T(8,128)(2,1)}, u32[]{:S(2)}) %copy-start) | copy-done | bytes 1048600
  2.4 43.3 %shard_map.100 = bf16[512,1024]{1,0:T(8,128)(2,1)S(1)} custom-call(bf16[512,1024]{1,0:T(8,128)(2,1)S(1)} %copy-done, bf16[128,512]{1,0:T(8,128)(2,1)S(1)} %reshape.7.wi_hbm, bf16[256,128]{1,0:T(8,128)(2,1)S(1)} %copy-done.1, f32[1,1024]{1,0:T(1,128)S(1)} %bitcast.6, bf16[31,1024]{1,0:T(8,128)(2,1)S(1)} %copy-done.2, f32[1,1024]{1,0:T(1,128)S(1)} %bitcast.7, ...), custom_call_target="tpu_custom_call" | custom-call | tf_op jit(solution)/shard_map/pallas_call | solution.py:543
  45.8 1.0 %copy.13 = bf16[512,1024]{1,0:T(8,128)(2,1)} copy(bf16[512,1024]{1,0:T(8,128)(2,1)S(1)} %shard_map.100) | data formatting | bytes 2097152
Async XLA Ops:
  0.0 1.1 %copy-start.1 = (bf16[256,128]{1,0:T(8,128)(2,1)S(1)}, bf16[256,128]{1,0:T(8,128)(2,1)}, u32[]{:S(2)}) copy-start(bf16[256,128]{1,0:T(8,128)(2,1)} %wo_hbm.1) | copy-start | bytes 196612
  0.0 1.1 %copy-start.2 = (bf16[31,1024]{1,0:T(8,128)(2,1)S(1)}, bf16[31,1024]{1,0:T(8,128)(2,1)}, u32[]{:S(2)}) copy-start(bf16[31,1024]{1,0:T(8,128)(2,1)} %taps.1) | copy-start | bytes 190468
  0.0 1.1 %copy-start.3 = (f32[1024]{0:T(1024)S(1)}, f32[1024]{0:T(1024)}, u32[]{:S(2)}) copy-start(f32[1024]{0:T(1024)} %param.11) | copy-start | bytes 12292
  0.0 1.1 %copy-start.4 = (f32[1024]{0:T(1024)S(1)}, f32[1024]{0:T(1024)}, u32[]{:S(2)}) copy-start(f32[1024]{0:T(1024)} %param.14) | copy-start | bytes 12292
  0.0 1.2 %copy-start.5 = (f32[1024]{0:T(1024)S(1)}, f32[1024]{0:T(1024)}, u32[]{:S(2)}) copy-start(f32[1024]{0:T(1024)} %param.15) | copy-start | bytes 12292
  0.0 1.2 %copy-start.6 = (s32[128]{0:T(128)S(1)}, s32[128]{0:T(128)}, u32[]{:S(2)}) copy-start(s32[128]{0:T(128)} %utts.1) | copy-start | bytes 1540
  0.0 1.2 %copy-start.7 = (s32[128]{0:T(128)S(1)}, s32[128]{0:T(128)}, u32[]{:S(2)}) copy-start(s32[128]{0:T(128)} %offs.1) | copy-start | bytes 1540
  0.0 1.2 %copy-start.8 = (s32[32]{0:T(128)S(1)}, s32[32]{0:T(128)}, u32[]{:S(2)}) copy-start(s32[32]{0:T(128)} %lens.1) | copy-start | bytes 388
  1.2 1.2 %copy-start = (bf16[512,1024]{1,0:T(8,128)(2,1)S(1)}, bf16[512,1024]{1,0:T(8,128)(2,1)}, u32[]{:S(2)}) copy-start(bf16[512,1024]{1,0:T(8,128)(2,1)} %frames_hbm.1) | copy-start | bytes 3145732
where the time goes:
time: 46.9 us; the launch traced here: 46.8 us
  Pallas kernels  43.3 us (92%)
  local copies, waits for them, and re-layouts  3.3 us (7%)
    pallas_call x1, Pallas kernels, fused_device(): pl.pallas_call(functools.partial(fused_kernel, nz), out_shape=jax.ShapeDt...  43.3 us
    unnamed x19, local copies, waits for them, and re-layouts  2.22 us
    reshape x1, local copies, waits for them, and re-layouts, fused_device(): w_in.reshape(krows, 2, groups, LANES).transpose(0, 2, 1, 3)  1.07 us

commit v1 on v0

v1 whole, which is shorter than its diff:
```python
import functools

import jax
import jax.numpy as jnp
from jax import lax
from jax.experimental import pallas as pl
from jax.experimental.pallas import tpu as pltpu
from jax.sharding import PartitionSpec as P

D = 1024
KER = 31
BLK = 128


epsilon = 1e-05


def extended(block, sides, width):
    for axis, dim in sides:
        count = lax.axis_size(axis)
        forward = [(i, i + 1) for i in range(count - 1)]
        backward = [(target, source) for source, target in forward]
        low = lax.ppermute(
            lax.slice_in_dim(block, block.shape[dim] - width, None, axis=dim), axis, forward
        )
        high = lax.ppermute(lax.slice_in_dim(block, 0, width, axis=dim), axis, backward)
        block = jnp.concatenate([low, block, high], axis=dim)
    return block


def frame_keys(block_utt, block_off, lengths, first_row, row_count, margin):
    places = first_row - margin + jnp.arange(row_count + 2 * margin, dtype=jnp.int32)
    total_rows = block_utt.shape[0] * BLK
    inside = (places >= 0) & (places < total_rows)
    blocks = jnp.clip(places // BLK, 0, block_utt.shape[0] - 1)
    utterance = jnp.take(block_utt, blocks)
    position = jnp.take(block_off, blocks) * BLK + places % BLK
    living = inside & (position < jnp.take(lengths, utterance))
    return (jnp.where(living, utterance, -1), living[margin : margin + row_count])


def layer_norm(rows, gain):
    values = rows.astype(jnp.float32)
    average = jnp.mean(values, axis=1, keepdims=True)
    centered = values - average
    spread = jnp.mean(centered * centered, axis=1, keepdims=True)
    return (centered * lax.rsqrt(spread + epsilon) * gain).astype(jnp.bfloat16)


def gate_units(projected, living):
    half = projected.shape[1] // 2
    values = projected[:, :half] * jax.nn.sigmoid(projected[:, half:])
    return (values * living.astype(jnp.float32)[:, None]).astype(jnp.bfloat16)


def depthwise(widened, keys_wide, taps, row_count):
    margin = (taps.shape[0] - 1) // 2
    center = keys_wide[margin : margin + row_count]
    summed = jnp.zeros((row_count, widened.shape[1]), jnp.float32)
    for tap_index in range(taps.shape[0]):
        shifted = widened[tap_index : tap_index + row_count].astype(jnp.float32)
        same = (keys_wide[tap_index : tap_index + row_count] == center)[:, None]
        summed = summed + jnp.where(same, shifted, 0.0) * taps[tap_index].astype(jnp.float32)
    return summed


def finish(mixed, stat_sum, square_sum, width_total, gain, bias):
    average = stat_sum / width_total
    spread = square_sum / width_total - average * average
    normed = (mixed - average[:, None]) * lax.rsqrt(spread + epsilon)[:, None] * gain + bias
    return (normed * jax.nn.sigmoid(normed)).astype(jnp.bfloat16)


def project_rows(normed, row_count, column_count):

    def add_rows(total, weight_piece, start_row):
        piece_rows = weight_piece.shape[0]
        return jnp.dot(
            normed, weight_piece.reshape(piece_rows, -1), preferred_element_type=jnp.float32
        )

    return (add_rows, jnp.zeros((row_count, column_count), jnp.float32))


def per_device(
    frames, ln1_gain, w_in, w_dw, ln2_gain, ln2_bias, w_out, block_utt, block_off, lengths
):
    row_count = frames.shape[0]
    margin = (KER - 1) // 2
    own_first = lax.axis_index(("seq", "grp")) * row_count
    keys_wide, living = frame_keys(block_utt, block_off, lengths, own_first, row_count, margin)
    normed = layer_norm(frames, ln1_gain)
    w_in_rows, w_out_rows = (
        lax.all_gather(w_in, "grp", axis=2, tiled=True),
        lax.all_gather(w_out, "grp", axis=0, tiled=True),
    )
    add_rows, empty = project_rows(normed, row_count, 2 * D)
    projected = add_rows(empty, lax.all_gather(w_in_rows, "seq", axis=0, tiled=True), jnp.int32(0))
    gated = gate_units(projected, living)
    widened = extended(gated, ((("seq", "grp"), 0),), margin)
    mixed = depthwise(widened, keys_wide, w_dw, row_count)
    act = finish(
        mixed, jnp.sum(mixed, axis=1), jnp.sum(mixed * mixed, axis=1), float(D), ln2_gain, ln2_bias
    )
    output = jnp.dot(
        act,
        lax.all_gather(w_out_rows, "seq", axis=1, tiled=True),
        preferred_element_type=jnp.float32,
    )
    alive = living.astype(jnp.float32)[:, None]
    return (frames.astype(jnp.float32) + output * alive).astype(jnp.bfloat16)


MESH = pl.DeviceIdType.MESH
HALO = 16
LANES = 128
PLANES = 4
O, X, Y, CX, CY, CZ, PP = (PLANES * i for i in range(7))
KINDS = 7 * PLANES + 8
COMPUTE = True

ORDER = (
    "Q0", "R0", "Q1", "N0", "XY00", "B00", "R1", "B01", "N1", "C00",
    "XY10", "Q2", "XY01", "B02", "B10", "B11", "G00", "halo", "K000", "C01",
    "D0", "C10", "L0", "XY11", "P00", "B12", "R2", "G10", "K010", "XY20",
    "L1", "C11", "D1", "G01", "K001", "B20", "L2", "P10", "B21", "K100",
    "C20", "G11", "P01", "XY21", "B22", "K011", "C21", "D2", "K110", "P11",
    "S0", "S1", "S2", "K101", "S3", "K111", "L3", "fin",
)


def fused_kernel(
    frames_hbm,
    wi_own,
    wo_own,
    gain1,
    taps,
    gain2,
    bias2,
    utts,
    offs,
    lens,
    out,
    WI,
    WO,
    FR,
    HB,
    NM,
    NH,
    GB0,
    GB1,
    MX,
    TP,
    ACT,
    S1,
    S2,
    limits,
    edge_limits,
    edge_joined,
    ssem,
    rsem,
    hs,
    hr,
    lsem,
):
    rows, width = FR.shape
    krows = wi_own.shape[0]
    nblk = rows // BLK
    chunks = width // LANES
    seq = lax.axis_index("seq")
    grp = lax.axis_index("grp")
    nseq = lax.axis_size("seq")
    ngrp = lax.axis_size("grp")
    z, y = seq // 2, seq % 2
    x, c = grp // 2, grp % 2
    index = seq * ngrp + grp
    total = nseq * ngrp
    hi, lo = z // 2, z % 2
    end = 1 - hi - lo + 2 * hi * lo
    near = 2 * hi + 1 - lo
    item_at = (z, 3 - z, near, 3 - near)
    source_at = (
        end * near + (1 - end) * (3 - z),
        end * (3 - z) + (1 - end) * near,
        3 - near,
    )

    px = (seq, (1 - x) * 2 + c)
    py = (z * 2 + 1 - y, grp)
    pp = (seq, x * 2 + 1 - c)
    has_next = index < total - 1
    has_before = index > 0
    after = jnp.minimum(index + 1, total - 1)
    before = jnp.maximum(index - 1, 0)
    pn = (after // ngrp, after % ngrp)
    pb = (before // ngrp, before % ngrp)

    def plane(t):
        return (t * 2 + y, grp)

    load = pltpu.make_async_copy(frames_hbm, FR, lsem.at[0])
    load.start()

    barrier = pltpu.get_barrier_semaphore()
    peers = [px, py, pp] + [plane((z + k) % PLANES) for k in range(1, PLANES)]
    for peer in peers:
        pl.semaphore_signal(barrier, inc=1, device_id=peer, device_id_type=MESH)

    @pl.when(has_next)
    def _():
        pl.semaphore_signal(barrier, inc=1, device_id=pn, device_id_type=MESH)

    @pl.when(has_before)
    def _():
        pl.semaphore_signal(barrier, inc=1, device_id=pb, device_id_type=MESH)

    @pl.when(jnp.logical_not(has_before))
    def _():
        HB[0] = jnp.zeros((HALO, width), jnp.bfloat16)

    @pl.when(jnp.logical_not(has_next))
    def _():
        HB[1] = jnp.zeros((HALO, width), jnp.bfloat16)

    own_rows = pl.ds(pl.multiple_of(seq * krows, krows), krows)
    for h in range(2):
        WI[h, c, x, own_rows, :] = wi_own[:, h * 2 * LANES : (h + 1) * 2 * LANES]
    WO[c, z, y, x] = wo_own[...]
    pl.semaphore_wait(
        barrier, len(peers) + has_next.astype(jnp.int32) + has_before.astype(jnp.int32)
    )

    def slot(w, sx, sy, sz, half=None):
        if w < 2:
            count = krows if half is None else krows // 2
            first = (sz * 2 + sy) * krows + (0 if half is None else half * count)
            return WI.at[w, c, sx, pl.ds(pl.multiple_of(first, count), count), :]
        if half is None:
            return WO.at[c, sz, sy, sx]
        count = WO.shape[4] // 2
        return WO.at[c, sz, sy, sx, pl.ds(half * count, count), :]

    sent = []
    middle_sent = []

    def copy(w, ref, sem, dev):
        return pltpu.make_async_remote_copy(
            src_ref=ref,
            dst_ref=ref,
            send_sem=ssem.at[w, len(sent) % KINDS],
            recv_sem=rsem.at[w, sem],
            device_id=dev,
            device_id_type=MESH,
        )

    count_of = [0, 0, 0]

    def send(w, ref, sem, dev):
        made = pltpu.make_async_remote_copy(
            src_ref=ref,
            dst_ref=ref,
            send_sem=ssem.at[w, count_of[w]],
            recv_sem=rsem.at[w, sem],
            device_id=dev,
            device_id_type=MESH,
        )
        made.start()
        count_of[w] += 1
        sent.append(made)

    def receive(w, ref, sem):
        copy(w, ref, sem, px).wait_recv()

    def middle_send(w, ref, sem, dev):
        made = pltpu.make_async_remote_copy(
            src_ref=ref,
            dst_ref=ref,
            send_sem=ssem.at[w, count_of[w]],
            recv_sem=rsem.at[w, sem],
            device_id=dev,
            device_id_type=MESH,
        )
        count_of[w] += 1
        middle_sent.append(made)

        @pl.when(end == 0)
        def _():
            made.start()

    def own_square(w):
        ref = slot(w, x, y, z)
        send(w, ref, X + z, px)
        send(w, ref, Y + z, py)

    def own_line(w):
        ref = slot(w, x, y, z)
        send(w, ref, O + z, plane(3 - z))
        send(w, ref, O + z, plane(near))

    def line(w, p):
        s = source_at[p]
        ref = slot(w, x, y, s)
        receive(w, ref, O + s)
        if p == 0:
            middle_send(w, slot(w, x, y, 3 - z), O + 3 - z, plane(near))
        if p == 1:
            middle_send(w, slot(w, x, y, near), O + near, plane(3 - z))
        send(w, ref, X + s, px)
        send(w, ref, Y + s, py)

    def corner_relay(w):
        ref = slot(w, 1 - x, 1 - y, near)
        receive(w, ref, CZ + near)
        middle_send(w, ref, CZ + near, plane(3 - z))

    def corner_sends(w, i):
        s = item_at[i]
        receive(w, slot(w, x, 1 - y, s), Y + s)
        send(w, slot(w, x, 1 - y, s, 0), CX + s, px)
        receive(w, slot(w, 1 - x, y, s), X + s)
        send(w, slot(w, 1 - x, y, s, 1), CY + s, py)

    def corner(w, i):
        s = item_at[i]
        receive(w, slot(w, 1 - x, 1 - y, s, 0), CX + s)
        receive(w, slot(w, 1 - x, 1 - y, s, 1), CY + s)
        if i == 0:
            send(w, slot(w, 1 - x, 1 - y, s), CZ + s, plane(near))
        else:
            middle_send(w, slot(w, 1 - x, 1 - y, s), CZ + s, plane(near))

    def group(w, rel):
        if rel == 0:
            for s in item_at[2:]:
                receive(w, slot(w, x, 1 - y, s), Y + s)
            send(w, WI.at[w, c, x], PP, pp)
        else:
            for s in item_at[2:]:
                receive(w, slot(w, 1 - x, y, s), X + s)
            receive(w, slot(w, 1 - x, 1 - y, 3 - near), CZ + 3 - near)
            send(w, WI.at[w, c, 1 - x], PP + 1, pp)

    def group_partner(w, rel):
        receive(w, WI.at[w, 1 - c, x if rel == 0 else 1 - x], PP + rel)

    def column(i):
        s = item_at[i]
        if i >= 2:
            receive(2, slot(2, x, 1 - y, s), Y + s)
            receive(2, slot(2, 1 - x, y, s), X + s)
        if i == 3:
            receive(2, slot(2, 1 - x, 1 - y, s), CZ + s)
        send(2, WO.at[c, s], PP + s, pp)

    def halo_copy(src, dst, sem, dev):
        return pltpu.make_async_remote_copy(
            src_ref=src,
            dst_ref=dst,
            send_sem=hs.at[sem],
            recv_sem=hr.at[sem],
            device_id=dev,
            device_id_type=MESH,
        )

    to_next = halo_copy(FR.at[pl.ds(rows - HALO, HALO), :], HB.at[0], 0, pn)
    to_before = halo_copy(FR.at[pl.ds(0, HALO), :], HB.at[1], 1, pb)

    def halo_start():
        @pl.when(has_next)
        def _():
            to_next.start()

        @pl.when(has_before)
        def _():
            to_before.start()

    def norm_rows(block):
        values = block.astype(jnp.float32)
        average = jnp.mean(values, axis=1, keepdims=True)
        centered = values - average
        spread_ = jnp.mean(centered * centered, axis=1, keepdims=True)
        return (centered * lax.rsqrt(spread_ + epsilon) * gain1[...]).astype(jnp.bfloat16)

    tall_rows = BLK
    pack = 2 * 8

    def tile(ref, first, ch):
        return ref[pl.ds(first, pack), ch * LANES : (ch + 1) * LANES].astype(jnp.float32)

    def row_sum(parts):
        total_ = parts[0]
        for part in parts[1:]:
            total_ = total_ + part
        return jnp.sum(total_, axis=1, keepdims=True)

    def norm(step):
        def bands(i):
            return [
                pl.multiple_of(i * tall_rows + r * pack, pack) for r in range(tall_rows // pack)
            ]

        def average_step(i, carry):
            for first in bands(i):
                average = row_sum([tile(FR, first, ch) for ch in range(chunks)]) / float(width)
                S1[pl.ds(first, pack), :] = jnp.broadcast_to(average, (pack, LANES))
            return carry

        def spread_step(i, carry):
            for first in bands(i):
                average = S1[pl.ds(first, pack), :]
                parts = [tile(FR, first, ch) - average for ch in range(chunks)]
                spread = row_sum([p * p for p in parts]) / float(width)
                scale = lax.rsqrt(spread + epsilon)
                S2[pl.ds(first, pack), :] = jnp.broadcast_to(scale, (pack, LANES))
            return carry

        def scale_step(i, carry):
            for first in bands(i):
                average = S1[pl.ds(first, pack), :]
                scale = S2[pl.ds(first, pack), :]
                for ch in range(chunks):
                    cols = slice(ch * LANES, (ch + 1) * LANES)
                    NM[pl.ds(first, pack), cols] = (
                        (tile(FR, first, ch) - average) * scale * gain1[:, cols]
                    ).astype(jnp.bfloat16)
            return carry

        count = rows // tall_rows // 2
        for stage in (average_step, spread_step, scale_step):
            lax.fori_loop(count * step, count * (step + 1), stage, 0)

    def halo():
        @pl.when(has_before)
        def _():
            to_next.wait_recv()

        @pl.when(has_next)
        def _():
            to_before.wait_recv()

        NH[0:HALO, :] = norm_rows(HB[0])
        NH[HALO:, :] = norm_rows(HB[1])

    first_block = index * nblk
    last_block = total * nblk - 1

    def block_info(b):
        u = utts[b]
        return u, lens[u] - offs[b] * BLK

    info = [
        block_info(jnp.clip(first_block + i, 0, last_block)) for i in range(-1, nblk + 1)
    ]
    joined = []
    for i in range(nblk + 1):
        same = info[i][0] == info[i + 1][0]
        if i == 0:
            same = same & (first_block > 0)
        if i == nblk:
            same = same & (first_block + nblk <= last_block)
        joined.append(same.astype(jnp.float32))
    alive_rows = [info[i + 1][1] for i in range(nblk)]
    for i in range(nblk):
        limits[i] = alive_rows[i]
    edge_limits[0] = info[0][1] - (BLK - HALO)
    edge_limits[1] = info[nblk + 1][1]
    edge_joined[0] = joined[0]
    edge_joined[1] = joined[nblk]

    def tall(count, start):
        return start + lax.broadcasted_iota(jnp.int32, (count, LANES), 0)

    stride = BLK + 2 * HALO

    def chunk_of(h, rel_c, rel_x):
        cc = c if rel_c == 0 else 1 - c
        xx = x if rel_x == 0 else 1 - x
        return cc, xx, (xx * 2 + cc) * 2 + h

    started = []
    pending = []
    deep = 4
    part_rows = 16 * deep
    parts = BLK // part_rows

    def convolve_step(j, ch, buf, fresh, tap):
        i, q = j // (2 * parts), j % (2 * parts)
        base = pl.multiple_of(i * stride + q * (8 * deep), 8)
        sums = [None] * deep
        for o in range(8 * (deep - 1) + KER):
            value = buf[pl.ds(base + (1 + o), 8), :]
            for t in range(deep):
                k = o - 8 * t
                if 0 <= k < KER:
                    term = value * tap[k]
                    sums[t] = term if sums[t] is None else sums[t] + term
        first = pl.multiple_of(j * (8 * deep), 8 * deep)
        for t in range(deep):
            band = pl.ds(pl.multiple_of(first + 8 * t, 8), 8)
            MX[ch, band, :] = sums[t]
            if fresh:
                S1[band, :] = sums[t]
                S2[band, :] = sums[t] * sums[t]
            else:
                S1[band, :] += sums[t]
                S2[band, :] += sums[t] * sums[t]

    def work(project_id):
        earlier = pending.pop() if pending else None
        if earlier is None and project_id is None:
            return
        if earlier is not None:
            old_ch, old_buf, fresh = earlier
            tap = [jnp.broadcast_to(TP[old_ch, k : k + 1, :], (8, LANES)) for k in range(KER)]
        if project_id is not None:
            h = project_id[0]
            cc, xx, ch = chunk_of(*project_id)
            buf = (GB0, GB1)[len(started) % 2]
            pending.append((ch, buf, not started))
            started.append(ch)

        def gated(p):
            half = 0.5 * p[:, :LANES]
            return half + half * jnp.tanh(0.5 * p[:, LANES:])

        def rounded(units):
            return units.astype(jnp.bfloat16).astype(jnp.float32)

        def at_once(between):
            lhs = jnp.concatenate([NM[...], NH[...]], axis=0)
            p = jnp.dot(lhs, WI[h, cc, xx], preferred_element_type=jnp.float32)
            between()
            units = gated(p)
            for i in range(nblk):
                main = jnp.where(tall(BLK, 0) < alive_rows[i], units[i * BLK : (i + 1) * BLK], 0.0)
                buf[i * stride + HALO : i * stride + HALO + BLK, :] = rounded(main)
            for q in range(2):
                strip = units[rows + q * HALO : rows + (q + 1) * HALO]
                strip = rounded(jnp.where(tall(HALO, 0) < edge_limits[q], strip, 0.0))
                place = q * (nblk * stride - HALO)
                buf[place : place + HALO, :] = strip * edge_joined[q]

        def convolve(steps):
            for j in steps:
                convolve_step(j, old_ch, old_buf, fresh, tap)

        count = 2 * nblk * parts
        if earlier is None:
            at_once(lambda: None)
        elif project_id is None:

            def step(j, carry):
                convolve((2 * j, 2 * j + 1))
                return carry

            lax.fori_loop(0, count // 2, step, 0)
        else:
            at_once(lambda: convolve(range(count)))
        if project_id is not None:
            for i in range(1, nblk):
                base = i * stride
                buf[base : base + HALO, :] = (
                    buf[base - 2 * HALO : base - HALO, :] * joined[i]
                )
                buf[base - HALO : base, :] = (
                    buf[base + HALO : base + 2 * HALO, :] * joined[i]
                )

    wide = 2 * LANES

    def finish_all():
        half = WO.shape[3] * WO.shape[4]
        for s in item_at:
            receive(2, WO.at[1 - c, s], PP + s)
        if not COMPUTE:
            return
        for b in range(nblk):
            stats = []
            for r in range(tall_rows // pack):
                band = slice(b * BLK + r * pack, b * BLK + (r + 1) * pack)
                average = jnp.sum(S1[band, :], axis=1, keepdims=True) / float(width)
                square = jnp.sum(S2[band, :], axis=1, keepdims=True) / float(width)
                scale = lax.rsqrt(square - average * average + epsilon)
                stats.append((band, average, scale))
            for ch in range(chunks):
                cols = slice(ch * LANES, (ch + 1) * LANES)
                g, h = ch // 2, ch % 2
                place = ((g % 2) * 2 + g // 2) * 2 + h
                half_gain = 0.5 * gain2[:, cols]
                half_bias = 0.5 * bias2[:, cols]
                for band, average, scale in stats:
                    v = (MX[ch, band, :] - average) * scale * half_gain + half_bias
                    ACT[band, place * LANES : (place + 1) * LANES] = (
                        v + v * jnp.tanh(v)
                    ).astype(jnp.bfloat16)
            band = slice(b * BLK, (b + 1) * BLK)
            lived = lax.broadcasted_iota(jnp.int32, (BLK, wide), 0) < alive_rows[b]
            for s in item_at:

                def side(sy):
                    return jnp.concatenate(
                        [WO[cc, s, sy].reshape(half, LANES) for cc in range(2)], axis=0
                    )

                weights = jnp.concatenate([side(0), side(1)], axis=1)
                o = jnp.dot(ACT[band, :], weights, preferred_element_type=jnp.float32)
                cols = pl.ds(pl.multiple_of(s * wide, wide), wide)
                out[band, cols] = (
                    FR[band, cols].astype(jnp.float32) + jnp.where(lived, o, 0.0)
                ).astype(jnp.bfloat16)

    for token in ORDER:
        arg = [int(d) for d in token if d.isdigit()]
        name = token.rstrip("0123456789")
        if name == "Q":
            own_square(*arg)
        elif name == "R":
            own_line(*arg)
            if arg[0] == 0:
                load.wait()
                halo_start()
                for ch in range(chunks):
                    TP[ch, 0:KER, :] = taps[:, ch * LANES : (ch + 1) * LANES].astype(
                        jnp.float32
                    )
        elif name == "B":
            line(*arg)
        elif name == "XY":
            corner_sends(*arg)
        elif name == "C":
            corner(*arg)
        elif name == "D":
            corner_relay(*arg)
        elif name == "G":
            group(arg[1], arg[0])
        elif name == "P":
            group_partner(arg[1], arg[0])
        elif name == "S":
            column(*arg)
        elif name == "fin":
            finish_all()
        elif name == "halo":
            halo()
        elif not COMPUTE:
            pass
        elif name == "K":
            work(arg)
        elif name == "L":
            work(None)
        elif name == "N":
            norm(*arg)

    if not COMPUTE:
        out[...] = FR[...]

    @pl.when(has_next)
    def _():
        to_next.wait_send()

    @pl.when(has_before)
    def _():
        to_before.wait_send()

    for made in sent:
        made.wait_send()

    @pl.when(end == 0)
    def _():
        for made in middle_sent:
            made.wait_send()


def fused_device(
    frames, ln1_gain, w_in, w_dw, ln2_gain, ln2_bias, w_out, block_utt, block_off, lengths
):
    rows, width = frames.shape
    nz = lax.axis_size("seq") // 2
    krows, _, cols = w_in.shape
    orows, ocols = w_out.shape
    groups = cols // LANES
    wi = w_in.reshape(krows, 2, groups, LANES).transpose(0, 2, 1, 3).reshape(krows, 2 * cols)
    vmem = pl.BlockSpec(memory_space=pltpu.VMEM)
    smem = pl.BlockSpec(memory_space=pltpu.SMEM)
    anywhere = pl.BlockSpec(memory_space=pl.ANY)
    nblk = rows // BLK
    return pl.pallas_call(
        fused_kernel,
        out_shape=jax.ShapeDtypeStruct((rows, width), jnp.bfloat16),
        in_specs=[anywhere] + [vmem] * 6 + [smem] * 3,
        out_specs=vmem,
        scratch_shapes=[
            pltpu.VMEM((2, 2, 2, width, 2 * LANES), jnp.bfloat16),
            pltpu.VMEM((2, nz, 2, 2, orows, ocols), jnp.bfloat16),
            pltpu.VMEM((rows, width), jnp.bfloat16),
            pltpu.VMEM((2, HALO, width), jnp.bfloat16),
            pltpu.VMEM((rows, width), jnp.bfloat16),
            pltpu.VMEM((2 * HALO, width), jnp.bfloat16),
            pltpu.VMEM((nblk * (BLK + 2 * HALO), LANES), jnp.float32),
            pltpu.VMEM((nblk * (BLK + 2 * HALO), LANES), jnp.float32),
            pltpu.VMEM((width // LANES, rows, LANES), jnp.float32),
            pltpu.VMEM((width // LANES, 32, LANES), jnp.float32),
            pltpu.VMEM((rows, width), jnp.bfloat16),
            pltpu.VMEM((rows, LANES), jnp.float32),
            pltpu.VMEM((rows, LANES), jnp.float32),
            pltpu.SMEM((nblk,), jnp.int32),
            pltpu.SMEM((2,), jnp.int32),
            pltpu.SMEM((2,), jnp.float32),
            pltpu.SemaphoreType.DMA((3, KINDS)),
            pltpu.SemaphoreType.DMA((3, KINDS)),
            pltpu.SemaphoreType.DMA((2,)),
            pltpu.SemaphoreType.DMA((2,)),
            pltpu.SemaphoreType.DMA((1,)),
        ],
        compiler_params=pltpu.CompilerParams(
            collective_id=0, has_side_effects=True, vmem_limit_bytes=52 << 20
        ),
    )(
        frames,
        wi,
        w_out,
        ln1_gain[None],
        w_dw,
        ln2_gain[None],
        ln2_bias[None],
        block_utt,
        block_off,
        lengths,
    )


def solution(mesh):
    seq, grp = mesh.shape["seq"], mesh.shape["grp"]
    fits = grp == 4 and seq == 2 * PLANES and D == grp * 2 * LANES

    return jax.shard_map(
        fused_device if fits else per_device,
        mesh=mesh,
        in_specs=(
            P(("seq", "grp"), None),
            P(),
            P("seq", None, "grp"),
            P(),
            P(),
            P(),
            P("grp", "seq"),
            P(),
            P(),
            P(),
        ),
        out_specs=P(("seq", "grp"), None),
        check_vma=False,
    )
```

time: 46.9 us -> 45.5 us (0.970)
  local copies, waits for them, and re-layouts: 3.3 us -> 2.08 us
    unnamed x19 -> x17, local copies, waits for them, and re-layouts: 2.22 us -> 1 us
where the time goes in v1:
time: 45.5 us; the launch traced here: 45.4 us
  Pallas kernels  43.2 us (95%)
  local copies, waits for them, and re-layouts  2.08 us (5%)
    pallas_call x1, Pallas kernels, fused_device(): pl.pallas_call(fused_kernel, out_shape=jax.ShapeDtypeStruct((rows, width)...  43.2 us
    reshape x1, local copies, waits for them, and re-layouts, fused_device(): w_in.reshape(krows, 2, groups, LANES).transpose(0, 2, 1, 3)  1.07 us
    unnamed x17, local copies, waits for them, and re-layouts  1 us

profile of v1, /device:TPU:0, one launch (start us, length us, event | category | flops | bytes accessed | tf_op | source)
XLA Modules:
  0.0 45.4 jit_solution(8832134535072867490)
XLA Ops:
  0.0 0.0 copy-start
  0.0 0.0 copy-start.1
  0.0 0.0 copy-start.2
  0.0 0.0 copy-start.3
  0.0 0.0 copy-start.4
  0.0 0.0 copy-start.5
  0.0 0.0 copy-start.6
  0.0 0.0 copy-start.7
  0.0 1.1 %reshape.7.wi_own = bf16[128,512]{1,0:T(8,128)(2,1)S(1)} reshape(bf16[128,2,2,128]{3,2,1,0:T(2,128)(2,1)} %bitcast.9) | data formatting | bytes 262144 | tf_op jit(solution)/shard_map/reshape | solution.py:681
  1.1 0.0 copy-done
  1.1 0.0 copy-done.1
  1.1 0.0 copy-done.2
  1.2 0.0 copy-done.3
  1.2 0.0 copy-done.4
  1.2 0.0 copy-done.5
  1.2 0.0 copy-done.6
  1.2 0.0 copy-done.7
  1.2 43.2 %shard_map.100 = bf16[512,1024]{1,0:T(8,128)(2,1)S(1)} custom-call(bf16[512,1024]{1,0:T(8,128)(2,1)} %frames_hbm.1, bf16[128,512]{1,0:T(8,128)(2,1)S(1)} %reshape.7.wi_own, bf16[256,128]{1,0:T(8,128)(2,1)S(1)} %copy-done, f32[1,1024]{1,0:T(1,128)S(1)} %bitcast.6, bf16[31,1024]{1,0:T(8,128)(2,1)S(1)} %copy-done.1, f32[1,1024]{1,0:T(1,128)S(1)} %bitcast.7, ...), custom_call_target="tpu_custom_call" | custom-call | tf_op jit(solution)/shard_map/pallas_call | solution.py:686
  44.4 1.0 %copy.13 = bf16[512,1024]{1,0:T(8,128)(2,1)} copy(bf16[512,1024]{1,0:T(8,128)(2,1)S(1)} %shard_map.100) | data formatting | bytes 2097152
Async XLA Ops:
  0.0 1.1 %copy-start = (bf16[256,128]{1,0:T(8,128)(2,1)S(1)}, bf16[256,128]{1,0:T(8,128)(2,1)}, u32[]{:S(2)}) copy-start(bf16[256,128]{1,0:T(8,128)(2,1)} %wo_own.1) | copy-start | bytes 196612
  0.0 1.1 %copy-start.1 = (bf16[31,1024]{1,0:T(8,128)(2,1)S(1)}, bf16[31,1024]{1,0:T(8,128)(2,1)}, u32[]{:S(2)}) copy-start(bf16[31,1024]{1,0:T(8,128)(2,1)} %taps.1) | copy-start | bytes 190468
  0.0 1.1 %copy-start.2 = (f32[1024]{0:T(1024)S(1)}, f32[1024]{0:T(1024)}, u32[]{:S(2)}) copy-start(f32[1024]{0:T(1024)} %param.11) | copy-start | bytes 12292
  0.0 1.1 %copy-start.3 = (f32[1024]{0:T(1024)S(1)}, f32[1024]{0:T(1024)}, u32[]{:S(2)}) copy-start(f32[1024]{0:T(1024)} %param.14) | copy-start | bytes 12292
  0.0 1.2 %copy-start.4 = (f32[1024]{0:T(1024)S(1)}, f32[1024]{0:T(1024)}, u32[]{:S(2)}) copy-start(f32[1024]{0:T(1024)} %param.15) | copy-start | bytes 12292
  0.0 1.2 %copy-start.5 = (s32[128]{0:T(128)S(1)}, s32[128]{0:T(128)}, u32[]{:S(2)}) copy-start(s32[128]{0:T(128)} %utts.1) | copy-start | bytes 1540
  0.0 1.2 %copy-start.6 = (s32[128]{0:T(128)S(1)}, s32[128]{0:T(128)}, u32[]{:S(2)}) copy-start(s32[128]{0:T(128)} %offs.1) | copy-start | bytes 1540
  0.0 1.2 %copy-start.7 = (s32[32]{0:T(128)S(1)}, s32[32]{0:T(128)}, u32[]{:S(2)}) copy-start(s32[32]{0:T(128)} %lens.1) | copy-start | bytes 388

commit v2 on v1

--- a/solution.py
+++ b/solution.py
@@ -121,11 +121,11 @@
 
 ORDER = (
     "Q0", "R0", "Q1", "N0", "XY00", "B00", "R1", "B01", "N1", "C00",
-    "XY10", "Q2", "XY01", "B02", "B10", "B11", "G00", "halo", "K000", "C01",
-    "D0", "C10", "L0", "XY11", "P00", "B12", "R2", "G10", "K010", "XY20",
-    "L1", "C11", "D1", "G01", "K001", "B20", "L2", "P10", "B21", "K100",
-    "C20", "G11", "P01", "XY21", "B22", "K011", "C21", "D2", "K110", "P11",
-    "S0", "S1", "S2", "K101", "S3", "K111", "L3", "fin",
+    "XY10", "Q2", "XY01", "B02", "B10", "B11", "R2", "C10", "C01", "D0",
+    "G00", "halo", "K000", "XY20", "B20", "XY11", "B12", "L0", "P00", "G10",
+    "K010", "C20", "B21", "C11", "D1", "L1", "G01", "K001", "XY21", "B22",
+    "P10", "K100", "G11", "C21", "D2", "P01", "K011", "S0", "S1", "S2",
+    "K110", "P11", "S3", "K101", "K111", "L3", "fin",
 )
 
 

time: 45.5 us -> 43.6 us (0.958)
  Pallas kernels: 43.2 us -> 41.3 us
    pallas_call x1, Pallas kernels: 43.2 us -> 41.3 us  [fused_device(): pl.pallas_call(fused_kernel, out_shape=jax.ShapeDtypeStruct((rows, width)...]
where the time goes in v2:
time: 43.6 us; the launch traced here: 43.4 us
  Pallas kernels  41.3 us (95%)
  local copies, waits for them, and re-layouts  2.08 us (5%)
    pallas_call x1, Pallas kernels, fused_device(): pl.pallas_call(fused_kernel, out_shape=jax.ShapeDtypeStruct((rows, width)...  41.3 us
    reshape x1, local copies, waits for them, and re-layouts, fused_device(): w_in.reshape(krows, 2, groups, LANES).transpose(0, 2, 1, 3)  1.07 us
    unnamed x17, local copies, waits for them, and re-layouts  1 us

profile of v2, /device:TPU:0, one launch (start us, length us, event | category | flops | bytes accessed | tf_op | source)
XLA Modules:
  0.0 43.4 jit_solution(4975684833563837190)
XLA Ops:
  0.0 0.0 copy-start
  0.0 0.0 copy-start.1
  0.0 0.0 copy-start.2
  0.0 0.0 copy-start.3
  0.0 0.0 copy-start.4
  0.0 0.0 copy-start.5
  0.0 0.0 copy-start.6
  0.0 0.0 copy-start.7
  0.0 1.1 %reshape.7.wi_own = bf16[128,512]{1,0:T(8,128)(2,1)S(1)} reshape(bf16[128,2,2,128]{3,2,1,0:T(2,128)(2,1)} %bitcast.9) | data formatting | bytes 262144 | tf_op jit(solution)/shard_map/reshape | solution.py:681
  1.1 0.0 copy-done
  1.1 0.0 copy-done.1
  1.1 0.0 copy-done.2
  1.2 0.0 copy-done.3
  1.2 0.0 copy-done.4
  1.2 0.0 copy-done.5
  1.2 0.0 copy-done.6
  1.2 0.0 copy-done.7
  1.2 41.3 %shard_map.100 = bf16[512,1024]{1,0:T(8,128)(2,1)S(1)} custom-call(bf16[512,1024]{1,0:T(8,128)(2,1)} %frames_hbm.1, bf16[128,512]{1,0:T(8,128)(2,1)S(1)} %reshape.7.wi_own, bf16[256,128]{1,0:T(8,128)(2,1)S(1)} %copy-done, f32[1,1024]{1,0:T(1,128)S(1)} %bitcast.6, bf16[31,1024]{1,0:T(8,128)(2,1)S(1)} %copy-done.1, f32[1,1024]{1,0:T(1,128)S(1)} %bitcast.7, ...), custom_call_target="tpu_custom_call" | custom-call | tf_op jit(solution)/shard_map/pallas_call | solution.py:686
  42.5 1.0 %copy.13 = bf16[512,1024]{1,0:T(8,128)(2,1)} copy(bf16[512,1024]{1,0:T(8,128)(2,1)S(1)} %shard_map.100) | data formatting | bytes 2097152
Async XLA Ops:
  0.0 1.1 %copy-start = (bf16[256,128]{1,0:T(8,128)(2,1)S(1)}, bf16[256,128]{1,0:T(8,128)(2,1)}, u32[]{:S(2)}) copy-start(bf16[256,128]{1,0:T(8,128)(2,1)} %wo_own.1) | copy-start | bytes 196612
  0.0 1.1 %copy-start.1 = (bf16[31,1024]{1,0:T(8,128)(2,1)S(1)}, bf16[31,1024]{1,0:T(8,128)(2,1)}, u32[]{:S(2)}) copy-start(bf16[31,1024]{1,0:T(8,128)(2,1)} %taps.1) | copy-start | bytes 190468
  0.0 1.1 %copy-start.2 = (f32[1024]{0:T(1024)S(1)}, f32[1024]{0:T(1024)}, u32[]{:S(2)}) copy-start(f32[1024]{0:T(1024)} %param.11) | copy-start | bytes 12292
  0.0 1.1 %copy-start.3 = (f32[1024]{0:T(1024)S(1)}, f32[1024]{0:T(1024)}, u32[]{:S(2)}) copy-start(f32[1024]{0:T(1024)} %param.14) | copy-start | bytes 12292
  0.0 1.2 %copy-start.4 = (f32[1024]{0:T(1024)S(1)}, f32[1024]{0:T(1024)}, u32[]{:S(2)}) copy-start(f32[1024]{0:T(1024)} %param.15) | copy-start | bytes 12292
  0.0 1.2 %copy-start.5 = (s32[128]{0:T(128)S(1)}, s32[128]{0:T(128)}, u32[]{:S(2)}) copy-start(s32[128]{0:T(128)} %utts.1) | copy-start | bytes 1540
  0.0 1.2 %copy-start.6 = (s32[128]{0:T(128)S(1)}, s32[128]{0:T(128)}, u32[]{:S(2)}) copy-start(s32[128]{0:T(128)} %offs.1) | copy-start | bytes 1540
  0.0 1.2 %copy-start.7 = (s32[32]{0:T(128)S(1)}, s32[32]{0:T(128)}, u32[]{:S(2)}) copy-start(s32[32]{0:T(128)} %lens.1) | copy-start | bytes 388

commit v3 on v2

--- a/solution.py
+++ b/solution.py
@@ -123,9 +123,9 @@
     "Q0", "R0", "Q1", "N0", "XY00", "B00", "R1", "B01", "N1", "C00",
     "XY10", "Q2", "XY01", "B02", "B10", "B11", "R2", "C10", "C01", "D0",
     "G00", "halo", "K000", "XY20", "B20", "XY11", "B12", "L0", "P00", "G10",
-    "K010", "C20", "B21", "C11", "D1", "L1", "G01", "K001", "XY21", "B22",
-    "P10", "K100", "G11", "C21", "D2", "P01", "K011", "S0", "S1", "S2",
-    "K110", "P11", "S3", "K101", "K111", "L3", "fin",
+    "K010", "C20", "B21", "L1", "C11", "D1", "G01", "K001", "XY21", "B22",
+    "P10", "K100", "G11", "K011", "C21", "D2", "P01", "S0", "S1", "S2",
+    "K110", "K101", "S3", "P11", "K111", "L3", "fin",
 )
 
 

time: 43.6 us -> 42.6 us (0.977)
  Pallas kernels: 41.3 us -> 40.3 us
    pallas_call x1, Pallas kernels: 41.3 us -> 40.3 us  [fused_device(): pl.pallas_call(fused_kernel, out_shape=jax.ShapeDtypeStruct((rows, width)...]
where the time goes in v3:
time: 42.6 us; the launch traced here: 42.5 us
  Pallas kernels  40.3 us (95%)
  local copies, waits for them, and re-layouts  2.08 us (5%)
    pallas_call x1, Pallas kernels, fused_device(): pl.pallas_call(fused_kernel, out_shape=jax.ShapeDtypeStruct((rows, width)...  40.3 us
    reshape x1, local copies, waits for them, and re-layouts, fused_device(): w_in.reshape(krows, 2, groups, LANES).transpose(0, 2, 1, 3)  1.07 us
    unnamed x17, local copies, waits for them, and re-layouts  1 us

profile of v3, /device:TPU:0, one launch (start us, length us, event | category | flops | bytes accessed | tf_op | source)
XLA Modules:
  0.0 42.5 jit_solution(12627372197943035016)
XLA Ops:
  0.0 0.0 copy-start
  0.0 0.0 copy-start.1
  0.0 0.0 copy-start.2
  0.0 0.0 copy-start.3
  0.0 0.0 copy-start.4
  0.0 0.0 copy-start.5
  0.0 0.0 copy-start.6
  0.0 0.0 copy-start.7
  0.0 1.1 %reshape.7.wi_own = bf16[128,512]{1,0:T(8,128)(2,1)S(1)} reshape(bf16[128,2,2,128]{3,2,1,0:T(2,128)(2,1)} %bitcast.9) | data formatting | bytes 262144 | tf_op jit(solution)/shard_map/reshape | solution.py:681
  1.1 0.0 copy-done
  1.1 0.0 copy-done.1
  1.1 0.0 copy-done.2
  1.2 0.0 copy-done.3
  1.2 0.0 copy-done.4
  1.2 0.0 copy-done.5
  1.2 0.0 copy-done.6
  1.2 0.0 copy-done.7
  1.2 40.3 %shard_map.100 = bf16[512,1024]{1,0:T(8,128)(2,1)S(1)} custom-call(bf16[512,1024]{1,0:T(8,128)(2,1)} %frames_hbm.1, bf16[128,512]{1,0:T(8,128)(2,1)S(1)} %reshape.7.wi_own, bf16[256,128]{1,0:T(8,128)(2,1)S(1)} %copy-done, f32[1,1024]{1,0:T(1,128)S(1)} %bitcast.6, bf16[31,1024]{1,0:T(8,128)(2,1)S(1)} %copy-done.1, f32[1,1024]{1,0:T(1,128)S(1)} %bitcast.7, ...), custom_call_target="tpu_custom_call" | custom-call | tf_op jit(solution)/shard_map/pallas_call | solution.py:686
  41.5 1.0 %copy.13 = bf16[512,1024]{1,0:T(8,128)(2,1)} copy(bf16[512,1024]{1,0:T(8,128)(2,1)S(1)} %shard_map.100) | data formatting | bytes 2097152
Async XLA Ops:
  0.0 1.1 %copy-start = (bf16[256,128]{1,0:T(8,128)(2,1)S(1)}, bf16[256,128]{1,0:T(8,128)(2,1)}, u32[]{:S(2)}) copy-start(bf16[256,128]{1,0:T(8,128)(2,1)} %wo_own.1) | copy-start | bytes 196612
  0.0 1.1 %copy-start.1 = (bf16[31,1024]{1,0:T(8,128)(2,1)S(1)}, bf16[31,1024]{1,0:T(8,128)(2,1)}, u32[]{:S(2)}) copy-start(bf16[31,1024]{1,0:T(8,128)(2,1)} %taps.1) | copy-start | bytes 190468
  0.0 1.1 %copy-start.2 = (f32[1024]{0:T(1024)S(1)}, f32[1024]{0:T(1024)}, u32[]{:S(2)}) copy-start(f32[1024]{0:T(1024)} %param.11) | copy-start | bytes 12292
  0.0 1.1 %copy-start.3 = (f32[1024]{0:T(1024)S(1)}, f32[1024]{0:T(1024)}, u32[]{:S(2)}) copy-start(f32[1024]{0:T(1024)} %param.14) | copy-start | bytes 12292
  0.0 1.2 %copy-start.4 = (f32[1024]{0:T(1024)S(1)}, f32[1024]{0:T(1024)}, u32[]{:S(2)}) copy-start(f32[1024]{0:T(1024)} %param.15) | copy-start | bytes 12292
  0.0 1.2 %copy-start.5 = (s32[128]{0:T(128)S(1)}, s32[128]{0:T(128)}, u32[]{:S(2)}) copy-start(s32[128]{0:T(128)} %utts.1) | copy-start | bytes 1540
  0.0 1.2 %copy-start.6 = (s32[128]{0:T(128)S(1)}, s32[128]{0:T(128)}, u32[]{:S(2)}) copy-start(s32[128]{0:T(128)} %offs.1) | copy-start | bytes 1540
  0.0 1.2 %copy-start.7 = (s32[32]{0:T(128)S(1)}, s32[32]{0:T(128)}, u32[]{:S(2)}) copy-start(s32[32]{0:T(128)} %lens.1) | copy-start | bytes 388
